TPU v7x, 32 devices: a whole 2x2x4 slice. The times are simulated.
32 devices in a mesh: row: 4 (over y, core), col: 8 (over z, x).
Axes of the slice: x: 2, y: 2, z: 4, core: 2. Of those that a mesh axis runs over, the one named last changes fastest.
Arguments:
- rhs: bfloat16 [6144, 6144], P('row', 'col'), may hold values from -6 to 6
- basis_left: bfloat16 [6144, 6144], P('col', 'row'), may hold values from -1 to 1, as said below
- basis_right: bfloat16 [6144, 6144], P('row', 'col'), may hold values from -1 to 1, as said below
- eig_left: float32 [6144], P('row'), may hold values from 0.1 to 4
- eig_right: float32 [6144], P('col'), may hold values from 0.1 to 4
Outputs:
- solution: bfloat16 [6144, 6144], P('col', 'row')
Inputs may be any that keep to these rules, and one draw needn't show every extreme that they name: `basis_left`: an orthogonal matrix drawn uniformly, rounded to bfloat16. `basis_right`: an orthogonal matrix drawn uniformly, rounded to bfloat16.
All inputs are finite; a program needn't handle non-finite values.
Results may differ from a plain program's by a relative error of at most 0.0085.
Values may be sent and summed in bfloat16 or wider, within the bound.
A program may use at most 128 MiB of HBM per device.

v0:
```python
import jax
import jax.numpy as jnp
from jax import lax
from jax.sharding import PartitionSpec as P


def body(rhs, basis_left, basis_right, eig_left, eig_right):
    c_strip = lax.all_gather(rhs, "row", axis=0, tiled=True)
    left_all = lax.all_gather(basis_left, "col", axis=0, tiled=True)
    first = lax.dot_general(
        left_all, c_strip, (((0,), (0,)), ((), ())), preferred_element_type=jnp.float32
    )
    projected = first.astype(jnp.bfloat16)
    right_strip = lax.all_gather(basis_right, "row", axis=0, tiled=True)
    chosen = right_strip
    second = jnp.dot(
        lax.all_gather(projected, "col", axis=1, tiled=True),
        chosen,
        preferred_element_type=jnp.float32,
    )
    scaled = (second / (eig_left[:, None] + eig_right[None, :])).astype(jnp.bfloat16)
    chosen = left_all
    half = lax.psum_scatter(
        jnp.dot(chosen, scaled, preferred_element_type=jnp.float32),
        "row",
        scatter_dimension=0,
        tiled=True,
    ).astype(jnp.bfloat16)
    half_all = lax.all_gather(half, "row", axis=0, tiled=True)
    chosen = half_all
    return lax.psum_scatter(
        lax.dot_general(
            chosen, basis_right, (((1,), (1,)), ((), ())), preferred_element_type=jnp.float32
        ),
        "col",
        scatter_dimension=0,
        tiled=True,
    ).astype(jnp.bfloat16)


def solution(mesh):
    in_specs = (P("row", "col"), P("col", "row"), P("row", "col"), P("row"), P("col"))
    out_specs = P("col", "row")
    return jax.shard_map(body, mesh=mesh, in_specs=in_specs, out_specs=out_specs, check_vma=False)
```

profile of v0, /device:TPU:0, one launch (start us, length us, event | category | flops | bytes accessed | tf_op | source)
XLA Modules:
  0.0 1751.5 jit_solution(14869084896472922109)
XLA Ops:
  6.5 0.0 all-gather.8.cloned.1.call-start
  6.5 0.7 all-gather.8.cloned.1.call-update
  7.3 0.0 all-gather.6.cloned.1.call-start
  7.3 0.7 all-gather.6.cloned.1.call-update
  8.0 0.0 all-gather.12.cloned.1.call-start
  8.1 0.7 all-gather.12.cloned.1.call-update
  8.7 0.0 copy-start.1
  8.8 0.0 copy-start.2
  8.8 0.0 all-gather.10.cloned.1.call-start
  8.8 67.1 %all-gather.8.cloned.1.call-done = bf16[6144,768]{1,0:T(8,128)(2,1)} async-done(((bf16[1536,768]{1,0:T(8,128)(2,1)}), bf16[6144,768]{1,0:T(8,128)(2,1)}) %all-gather.8.cloned.1.call-update) | async-done | bytes 9437200 | tf_op jit(solution)/shard_map/all_gather | solution.py:8
  75.9 364.0 %all-gather.6.cloned.1.call-done = bf16[6144,1536]{1,0:T(8,128)(2,1)} async-done(((bf16[768,1536]{1,0:T(8,128)(2,1)}), bf16[6144,1536]{1,0:T(8,128)(2,1)}) %all-gather.6.cloned.1.call-update) | async-done | bytes 18874384 | tf_op jit(solution)/shard_map/all_gather | solution.py:9
  439.8 21.5 %convolution_convert_fusion = bf16[1536,768]{1,0:T(8,128)(2,1)} fusion(bf16[6144,1536]{1,0:T(8,128)(2,1)} %all-gather.6.cloned.1.call-done, bf16[6144,768]{1,0:T(8,128)(2,1)} %all-gather.8.cloned.1.call-done), kind=kOutput, calls=%fused_computation.2 | convolution fusion | flops 14496694272 | bytes 30670848 | tf_op jit(solution)/shard_map/dot_general | solution.py:10
  461.3 0.0 all-gather.10.cloned.1.call-update
  461.3 0.2 reduce-scatter.3.cloned.1.call-start
  461.5 44.1 %all-gather.12.cloned.1.call-done = bf16[6144,768]{1,0:T(8,128)(2,1)} async-done(((bf16[1536,768]{1,0:T(8,128)(2,1)}), bf16[6144,768]{1,0:T(8,128)(2,1)}) %all-gather.12.cloned.1.call-update) | async-done | bytes 9437200 | tf_op jit(solution)/shard_map/all_gather | solution.py:14
  505.6 363.8 %all-gather.10.cloned.1.call-done = bf16[1536,6144]{1,0:T(8,128)(2,1)} async-done(((bf16[1536,768]{1,0:T(8,128)(2,1)}), bf16[1536,6144]{1,0:T(8,128)(2,1)}) %all-gather.10.cloned.1.call-update) | async-done | bytes 18874384 | tf_op jit(solution)/shard_map/all_gather | solution.py:17
  869.4 0.0 copy-done.1
  869.4 0.0 copy-done.2
  869.4 20.6 %divide_convert_fusion = bf16[1536,768]{1,0:T(8,128)(2,1)S(1)} fusion(bf16[1536,6144]{1,0:T(8,128)(2,1)} %all-gather.10.cloned.1.call-done, bf16[6144,768]{1,0:T(8,128)(2,1)} %all-gather.12.cloned.1.call-done, f32[768]{0:T(1024)S(1)} %copy-done.2, f32[1536]{0:T(1024)S(1)} %copy-done.1), kind=kOutput, calls=%fused_computation.1 | convolution fusion | flops 14499053568 | bytes 30680064 | tf_op jit(solution)/shard_map/dot_general | solution.py:16
  890.1 20.7 %convolution_bitcast_fusion = f32[6144,768]{0,1:T(8,128)} fusion(bf16[1536,768]{1,0:T(8,128)(2,1)S(1)} %divide_convert_fusion, bf16[6144,1536]{1,0:T(8,128)(2,1)} %all-gather.6.cloned.1.call-done), kind=kOutput, calls=%fused_computation | convolution fusion | flops 14495514624 | bytes 40108032 | tf_op jit(solution)/shard_map/dot_general | solution.py:24
  910.8 0.0 reduce-scatter.3.cloned.1.call-update
  910.8 0.0 copy-start
  910.8 0.0 all-gather.14.cloned.1.call-start
  910.9 137.8 %reduce-scatter.3.cloned.1.call-done = f32[1536,768]{0,1:T(8,128)} async-done(((f32[6144,768]{0,1:T(8,128)}), f32[1536,768]{0,1:T(8,128)}) %reduce-scatter.3.cloned.1.call-update) | async-done | bytes 4718608 | tf_op jit(solution)/shard_map/reduce_scatter | solution.py:23
  1048.7 4.0 convert_element_type.14
  1052.7 0.0 all-gather.14.cloned.1.call-update
  1052.7 0.3 reduce-scatter.5.cloned.1.call-start
  1053.0 64.1 %all-gather.14.cloned.1.call-done = bf16[6144,768]{0,1:T(8,128)(2,1)} async-done(((bf16[1536,768]{0,1:T(8,128)(2,1)}), bf16[6144,768]{0,1:T(8,128)(2,1)}) %all-gather.14.cloned.1.call-update) | async-done | bytes 9437200 | tf_op jit(solution)/shard_map/all_gather | solution.py:29
  1117.1 22.7 %fusion = f32[6144,1536]{1,0:T(8,128)} fusion(bf16[6144,768]{0,1:T(8,128)(2,1)} %all-gather.14.cloned.1.call-done, bf16[1536,768]{1,0:T(8,128)(2,1)S(1)} %copy-done), kind=kOutput, calls=%fused_computation.3 | convolution fusion | flops 14495514624 | bytes 49545216 | tf_op jit(solution)/shard_map/dot_general | solution.py:32
  1139.8 0.0 reduce-scatter.5.cloned.1.call-update
  1139.8 600.8 %reduce-scatter.5.cloned.1.call-done = f32[768,1536]{1,0:T(8,128)} async-done(((f32[6144,1536]{1,0:T(8,128)}), f32[768,1536]{1,0:T(8,128)}) %reduce-scatter.5.cloned.1.call-update) | async-done | bytes 4718608 | tf_op jit(solution)/shard_map/reduce_scatter | solution.py:31
  1740.6 4.0 convert_element_type.15
  (1 shorter events, 0.0 us)
Async XLA Ops:
  6.5 69.3 %all-gather.8.cloned.1.call-start = ((), (), s32[]{:S(2)}) async-start(), calls=%async_computation.3 | async-start | bytes 11796480 | tf_op jit(solution)/shard_map/all_gather | solution.py:8
  7.3 432.6 %all-gather.6.cloned.1.call-start = ((), (), s32[]{:S(2)}) async-start(), calls=%async_computation.2 | async-start | bytes 21233664 | tf_op jit(solution)/shard_map/all_gather | solution.py:9
  8.0 497.6 %all-gather.12.cloned.1.call-start = ((), (), s32[]{:S(2)}) async-start(), calls=%async_computation.5 | async-start | bytes 11796480 | tf_op jit(solution)/shard_map/all_gather | solution.py:14
  8.7 860.7 %copy-start.1 = (f32[1536]{0:T(1024)S(1)}, f32[1536]{0:T(1024)}, u32[]{:S(2)}) copy-start(f32[1536]{0:T(1024)} %param.8) | copy-start | bytes 18436
  8.8 860.7 %copy-start.2 = (f32[768]{0:T(1024)S(1)}, f32[768]{0:T(1024)}, u32[]{:S(2)}) copy-start(f32[768]{0:T(1024)} %param.9) | copy-start | bytes 9220
  8.8 860.7 %all-gather.10.cloned.1.call-start = ((), (), s32[]{:S(2)}) async-start(), calls=%async_computation.4 | async-start | bytes 21233664 | tf_op jit(solution)/shard_map/all_gather | solution.py:17
  461.3 587.4 %reduce-scatter.3.cloned.1.call-start = ((), (), s32[]{:S(2)}) async-start(), calls=%async_computation.6 | async-start | bytes 23592960 | tf_op jit(solution)/shard_map/reduce_scatter | solution.py:23
  910.8 206.3 %copy-start = (bf16[1536,768]{1,0:T(8,128)(2,1)S(1)}, bf16[1536,768]{1,0:T(8,128)(2,1)}, u32[]{:S(2)}) copy-start(bf16[1536,768]{1,0:T(8,128)(2,1)} %param.7) | copy-start | bytes 7077892
  910.8 206.3 %all-gather.14.cloned.1.call-start = ((), (), s32[]{:S(2)}) async-start(), calls=%async_computation.7 | async-start | bytes 11796480 | tf_op jit(solution)/shard_map/all_gather | solution.py:29
  1052.7 687.9 %reduce-scatter.5.cloned.1.call-start = ((), (), s32[]{:S(2)}) async-start(), calls=%async_computation.8 | async-start | bytes 42467328 | tf_op jit(solution)/shard_map/reduce_scatter | solution.py:31
Sparse Core Ops, SparseCore 0:
  8.9 66.9 all-gather.7
  77.4 362.3 all-gather.5
  441.4 64.1 all-gather.11
  507.0 362.3 all-gather.9
  910.9 137.7 reduce-scatter.2
  1052.8 64.2 all-gather.13
  1139.9 600.6 reduce-scatter.4
where the time goes:
time: 1750 us
  waiting for transfers between devices  1640 us (94%)
  matrix products  85.5 us (5%)
    reduce_scatter x1, waiting for transfers between devices, body(): lax.psum_scatter(lax.dot_general(chosen, basis_right, (((1,), (1,)), ((),...  601 us
    all_gather x1, waiting for transfers between devices, body(): left_all = lax.all_gather(basis_left, 'col', axis=0, tiled=True)  364 us
    all_gather x1, waiting for transfers between devices, body(): lax.all_gather(projected, 'col', axis=1, tiled=True)  364 us
    reduce_scatter x1, waiting for transfers between devices, body(): lax.psum_scatter(jnp.dot(chosen, scaled, preferred_element_type=jnp.float...  138 us
    all_gather x1, waiting for transfers between devices, body(): c_strip = lax.all_gather(rhs, 'row', axis=0, tiled=True)  67.1 us
    all_gather x1, waiting for transfers between devices, body(): half_all = lax.all_gather(half, 'row', axis=0, tiled=True)  64.1 us
    all_gather x1, waiting for transfers between devices, body(): right_strip = lax.all_gather(basis_right, 'row', axis=0, tiled=True)  44.1 us
  transfers between devices with their start and end apart: 7, of which 7 were waited for; matrix products, arithmetic and copies ran while one was open for 1% of the time, Pallas kernels for 0%

commit v1 on v0

--- a/solution.py
+++ b/solution.py
@@ -6,7 +6,12 @@
 
 def body(rhs, basis_left, basis_right, eig_left, eig_right):
     c_strip = lax.all_gather(rhs, "row", axis=0, tiled=True)
-    left_all = lax.all_gather(basis_left, "col", axis=0, tiled=True)
+    ring = [basis_left]
+    for hop in range(7):
+        ring.append(lax.ppermute(ring[-1], "col", [(dev, (dev + 1) % 8) for dev in range(8)]))
+    left_all = jnp.roll(
+        jnp.concatenate(ring[::-1], axis=0), (lax.axis_index("col") + 1) * ring[0].shape[0], axis=0
+    )
     first = lax.dot_general(
         left_all, c_strip, (((0,), (0,)), ((), ())), preferred_element_type=jnp.float32
     )

time: 1750 us -> 1690 us (0.966)
  waiting for transfers between devices: 1640 us -> 1540 us
  local copies, waits for them, and re-layouts: 0.01 us -> 44.7 us
    ppermute x0 -> x7, waiting for transfers between devices: none -> 373 us  [body(): lax.ppermute(ring[-1], 'col', [(dev, (dev + 1) % 8) for dev in range(8)])]
    all_gather x1 -> x0, waiting for transfers between devices: 364 us -> none  [body(): left_all = lax.all_gather(basis_left, 'col', axis=0, tiled=True)]
    all_gather x1, waiting for transfers between devices: 67.1 us -> 0.01 us  [body(): c_strip = lax.all_gather(rhs, 'row', axis=0, tiled=True)]
    all_gather x1, waiting for transfers between devices: 44.1 us -> 0.02 us  [body(): right_strip = lax.all_gather(basis_right, 'row', axis=0, tiled=True)]
    unnamed x6 -> x35, local copies, waits for them, and re-layouts: 0.01 us -> 43.1 us
  transfers between devices with their start and end apart: 7 -> 13, of which waited for: 7 -> 11; matrix products, arithmetic and copies ran while one was open for 1% -> 4% of each run, Pallas kernels for 0% -> 0%
where the time goes in v1:
time: 1690 us
  waiting for transfers between devices  1540 us (91%)
  matrix products  86 us (5%)
  local copies, waits for them, and re-layouts  44.7 us (3%)
    reduce_scatter x1, waiting for transfers between devices, body(): lax.psum_scatter(lax.dot_general(chosen, basis_right, (((1,), (1,)), ((),...  601 us
    ppermute x7, waiting for transfers between devices, body(): lax.ppermute(ring[-1], 'col', [(dev, (dev + 1) % 8) for dev in range(8)])  373 us
    all_gather x1, waiting for transfers between devices, body(): lax.all_gather(projected, 'col', axis=1, tiled=True)  358 us
    reduce_scatter x1, waiting for transfers between devices, body(): lax.psum_scatter(jnp.dot(chosen, scaled, preferred_element_type=jnp.float...  138 us
    all_gather x1, waiting for transfers between devices, body(): half_all = lax.all_gather(half, 'row', axis=0, tiled=True)  64.1 us
    unnamed x35, local copies, waits for them, and re-layouts  43.1 us
  transfers between devices with their start and end apart: 13, of which 11 were waited for; matrix products, arithmetic and copies ran while one was open for 4% of the time, Pallas kernels for 0%

profile of v1, /device:TPU:0, one launch (start us, length us, event | category | flops | bytes accessed | tf_op | source)
XLA Modules:
  0.0 1691.3 jit_solution(4801309569217623508)
XLA Ops:
  7.3 3.0 collective-permute-start
  10.3 54.5 %collective-permute-done = bf16[768,1536]{1,0:T(8,128)(2,1)S(1)} collective-permute-done((bf16[768,1536]{1,0:T(8,128)(2,1)}, bf16[768,1536]{1,0:T(8,128)(2,1)S(1)}, u32[]{:S(2)}, u32[]{:S(2)}) %collective-permute-start) | collective-permute-done | bytes 2359328 | tf_op jit(solution)/shard_map/ppermute | solution.py:11
  66.3 55.1 %collective-permute-done.1 = bf16[768,1536]{1,0:T(8,128)(2,1)S(1)} collective-permute-done((bf16[768,1536]{1,0:T(8,128)(2,1)S(1)}, bf16[768,1536]{1,0:T(8,128)(2,1)S(1)}, u32[]{:S(2)}, u32[]{:S(2)}) %collective-permute-start.1) | collective-permute-done | bytes 2359328 | tf_op jit(solution)/shard_map/ppermute | solution.py:11
  122.8 54.4 %collective-permute-done.2 = bf16[768,1536]{1,0:T(8,128)(2,1)} collective-permute-done((bf16[768,1536]{1,0:T(8,128)(2,1)S(1)}, bf16[768,1536]{1,0:T(8,128)(2,1)}, u32[]{:S(2)}, u32[]{:S(2)}) %collective-permute-start.2) | collective-permute-done | bytes 2359328 | tf_op jit(solution)/shard_map/ppermute | solution.py:11
  177.2 53.6 %collective-permute-done.3 = bf16[768,1536]{1,0:T(8,128)(2,1)} collective-permute-done((bf16[768,1536]{1,0:T(8,128)(2,1)}, bf16[768,1536]{1,0:T(8,128)(2,1)}, u32[]{:S(2)}, u32[]{:S(2)}) %collective-permute-start.3) | collective-permute-done | bytes 2359328 | tf_op jit(solution)/shard_map/ppermute | solution.py:11
  230.9 52.7 %collective-permute-done.4 = bf16[768,1536]{1,0:T(8,128)(2,1)S(1)} collective-permute-done((bf16[768,1536]{1,0:T(8,128)(2,1)}, bf16[768,1536]{1,0:T(8,128)(2,1)S(1)}, u32[]{:S(2)}, u32[]{:S(2)}) %collective-permute-start.4) | collective-permute-done | bytes 2359328 | tf_op jit(solution)/shard_map/ppermute | solution.py:11
  285.0 51.8 %collective-permute-done.5 = bf16[768,1536]{1,0:T(8,128)(2,1)} collective-permute-done((bf16[768,1536]{1,0:T(8,128)(2,1)S(1)}, bf16[768,1536]{1,0:T(8,128)(2,1)}, u32[]{:S(2)}, u32[]{:S(2)}) %collective-permute-start.5) | collective-permute-done | bytes 2359328 | tf_op jit(solution)/shard_map/ppermute | solution.py:11
  336.8 51.1 %collective-permute-done.6 = bf16[768,1536]{1,0:T(8,128)(2,1)} collective-permute-done((bf16[768,1536]{1,0:T(8,128)(2,1)}, bf16[768,1536]{1,0:T(8,128)(2,1)}, u32[]{:S(2)}, u32[]{:S(2)}) %collective-permute-start.6) | collective-permute-done | bytes 2359328 | tf_op jit(solution)/shard_map/ppermute | solution.py:11
  387.9 3.2 constant_dynamic-update-slice_fusion.15
  391.2 3.3 constant_dynamic-update-slice_fusion.14
  394.5 3.4 constant_dynamic-update-slice_fusion.13
  397.9 3.3 constant_dynamic-update-slice_fusion.12
  401.2 3.2 constant_dynamic-update-slice_fusion.11
  404.4 1.6 constant_dynamic-update-slice_fusion.10
  407.5 1.6 constant_dynamic-update-slice_fusion.8
  409.1 3.2 constant_dynamic-update-slice_fusion.7
  412.3 3.3 constant_dynamic-update-slice_fusion.6
  415.6 1.6 constant_dynamic-update-slice_fusion.5
  417.2 3.2 constant_dynamic-update-slice_fusion.4
  420.4 3.3 constant_dynamic-update-slice_fusion.3
  423.7 1.6 constant_dynamic-update-slice_fusion.2
  426.8 1.6 constant_dynamic-update-slice_fusion
  428.4 21.5 %fusion.4 = bf16[1536,768]{1,0:T(8,128)(2,1)} fusion(bf16[6144,768]{1,0:T(8,128)(2,1)} %all-gather.5.cloned.1.call-done, bf16[12288,1536]{1,0:T(8,128)(2,1)} %constant_dynamic-update-slice_fusion, s32[]{:T(128)S(6)} %select_n.14), kind=kOutput, calls=%fused_computation.5 | convolution fusion | flops 14496694272 | bytes 30670852 | tf_op jit(solution)/shard_map/dot_general | solution.py:15
  450.2 358.4 %all-gather.7.cloned.1.call-done = bf16[1536,6144]{1,0:T(8,128)(2,1)} async-done(((bf16[1536,768]{1,0:T(8,128)(2,1)}), bf16[1536,6144]{1,0:T(8,128)(2,1)}) %all-gather.7.cloned.1.call-update) | async-done | bytes 18874384 | tf_op jit(solution)/shard_map/all_gather | solution.py:22
  808.7 20.6 %divide_convert_fusion = bf16[1536,768]{1,0:T(8,128)(2,1)S(1)} fusion(bf16[1536,6144]{1,0:T(8,128)(2,1)} %all-gather.7.cloned.1.call-done, bf16[6144,768]{1,0:T(8,128)(2,1)} %all-gather.9.cloned.1.call-done, f32[768]{0:T(1024)S(1)} %copy-done.9, f32[1536]{0:T(1024)S(1)} %copy-done.8), kind=kOutput, calls=%fused_computation.4 | convolution fusion | flops 14499053568 | bytes 30680064 | tf_op jit(solution)/shard_map/dot_general | solution.py:21
  829.3 21.3 %fusion = f32[6144,768]{1,0:T(8,128)} fusion(bf16[1536,768]{1,0:T(8,128)(2,1)S(1)} %divide_convert_fusion, bf16[12288,1536]{1,0:T(8,128)(2,1)} %constant_dynamic-update-slice_fusion, s32[]{:T(128)S(6)} %select_n.14), kind=kOutput, calls=%fused_computation | convolution fusion | flops 14495514624 | bytes 40108036 | tf_op jit(solution)/shard_map/dot_general | solution.py:29
  850.7 137.9 %reduce-scatter.3.cloned.1.call-done = f32[1536,768]{1,0:T(8,128)} async-done(((f32[6144,768]{1,0:T(8,128)}), f32[1536,768]{1,0:T(8,128)}) %reduce-scatter.3.cloned.1.call-update) | async-done | bytes 4718608 | tf_op jit(solution)/shard_map/reduce_scatter | solution.py:28
  988.6 4.0 convert_element_type.14
  992.8 64.1 %all-gather.11.cloned.1.call-done = bf16[6144,768]{1,0:T(8,128)(2,1)} async-done(((bf16[1536,768]{1,0:T(8,128)(2,1)}), bf16[6144,768]{1,0:T(8,128)(2,1)}) %all-gather.11.cloned.1.call-update) | async-done | bytes 9437200 | tf_op jit(solution)/shard_map/all_gather | solution.py:34
  1056.9 22.6 %fusion.9 = f32[6144,1536]{1,0:T(8,128)} fusion(bf16[6144,768]{1,0:T(8,128)(2,1)} %all-gather.11.cloned.1.call-done, bf16[1536,768]{1,0:T(8,128)(2,1)S(1)} %copy-done.7), kind=kOutput, calls=%fused_computation.24 | convolution fusion | flops 14495514624 | bytes 49545216 | tf_op jit(solution)/shard_map/dot_general | solution.py:37
  1079.5 600.9 %reduce-scatter.5.cloned.1.call-done = f32[768,1536]{1,0:T(8,128)} async-done(((f32[6144,1536]{1,0:T(8,128)}), f32[768,1536]{1,0:T(8,128)}) %reduce-scatter.5.cloned.1.call-update) | async-done | bytes 4718608 | tf_op jit(solution)/shard_map/reduce_scatter | solution.py:36
  1680.5 4.0 convert_element_type.15
  (42 shorter events, 8.8 us)
Async XLA Ops:
  6.5 401.0 %copy-start = (bf16[768,1536]{1,0:T(8,128)(2,1)S(1)}, bf16[768,1536]{1,0:T(8,128)(2,1)}, u32[]{:S(2)}) copy-start(bf16[768,1536]{1,0:T(8,128)(2,1)} %param.6) | copy-start | bytes 7077892
  6.5 421.9 %all-gather.5.cloned.1.call-start = ((), (), s32[]{:S(2)}) async-start(), calls=%async_computation.2 | async-start | bytes 11796480 | tf_op jit(solution)/shard_map/all_gather | solution.py:8
  7.3 443.0 %all-gather.9.cloned.1.call-start = ((), (), s32[]{:S(2)}) async-start(), calls=%async_computation.4 | async-start | bytes 11796480 | tf_op jit(solution)/shard_map/all_gather | solution.py:19
  7.3 57.5 %collective-permute-start = (bf16[768,1536]{1,0:T(8,128)(2,1)}, bf16[768,1536]{1,0:T(8,128)(2,1)S(1)}, u32[]{:S(2)}, u32[]{:S(2)}) collective-permute-start(bf16[768,1536]{1,0:T(8,128)(2,1)} %param.6), channel_id=1, source_target_pairs={{0,1},{1,2},{2,3},{3,4},{4,5},{5,6},{6,7},{7,0},{8,9},{9,10},{10,1... | collective-permute-start | bytes 7077896 | tf_op jit(solution)/shard_map/ppermute | solution.py:11
  64.8 1.4 copy-start.1
  66.3 55.1 %collective-permute-start.1 = (bf16[768,1536]{1,0:T(8,128)(2,1)S(1)}, bf16[768,1536]{1,0:T(8,128)(2,1)S(1)}, u32[]{:S(2)}, u32[]{:S(2)}) collective-permute-start(bf16[768,1536]{1,0:T(8,128)(2,1)S(1)} %collective-permute-done), channel_id=1, source_target_pairs={{0,1},{1,2},{2,3},{3,4},{4,5},{5,6},{6,7},{7,0},{8,9},{9,10},{10,1... | collective-permute-start | bytes 7077896 | tf_op jit(solution)/shard_map/ppermute | solution.py:11
  121.4 1.4 copy-start.3
  122.8 54.4 %collective-permute-start.2 = (bf16[768,1536]{1,0:T(8,128)(2,1)S(1)}, bf16[768,1536]{1,0:T(8,128)(2,1)}, u32[]{:S(2)}, u32[]{:S(2)}) collective-permute-start(bf16[768,1536]{1,0:T(8,128)(2,1)S(1)} %collective-permute-done.1), channel_id=1, source_target_pairs={{0,1},{1,2},{2,3},{3,4},{4,5},{5,6},{6,7},{7,0},{8,9},{9,10},{10,1... | collective-permute-start | bytes 7077896 | tf_op jit(solution)/shard_map/ppermute | solution.py:11
  177.1 53.7 %collective-permute-start.3 = (bf16[768,1536]{1,0:T(8,128)(2,1)}, bf16[768,1536]{1,0:T(8,128)(2,1)}, u32[]{:S(2)}, u32[]{:S(2)}) collective-permute-start(bf16[768,1536]{1,0:T(8,128)(2,1)} %collective-permute-done.2), channel_id=1, source_target_pairs={{0,1},{1,2},{2,3},{3,4},{4,5},{5,6},{6,7},{7,0},{8,9},{9,10},{10,1... | collective-permute-start | bytes 7077896 | tf_op jit(solution)/shard_map/ppermute | solution.py:11
  177.2 631.5 %all-gather.7.cloned.1.call-start = ((), (), s32[]{:S(2)}) async-start(), calls=%async_computation.3 | async-start | bytes 21233664 | tf_op jit(solution)/shard_map/all_gather | solution.py:22
  230.8 52.8 %collective-permute-start.4 = (bf16[768,1536]{1,0:T(8,128)(2,1)}, bf16[768,1536]{1,0:T(8,128)(2,1)S(1)}, u32[]{:S(2)}, u32[]{:S(2)}) collective-permute-start(bf16[768,1536]{1,0:T(8,128)(2,1)} %collective-permute-done.3), channel_id=1, source_target_pairs={{0,1},{1,2},{2,3},{3,4},{4,5},{5,6},{6,7},{7,0},{8,9},{9,10},{10,1... | collective-permute-start | bytes 7077896 | tf_op jit(solution)/shard_map/ppermute | solution.py:11
  283.6 1.4 copy-start.5
  285.0 51.8 %collective-permute-start.5 = (bf16[768,1536]{1,0:T(8,128)(2,1)S(1)}, bf16[768,1536]{1,0:T(8,128)(2,1)}, u32[]{:S(2)}, u32[]{:S(2)}) collective-permute-start(bf16[768,1536]{1,0:T(8,128)(2,1)S(1)} %collective-permute-done.4), channel_id=1, source_target_pairs={{0,1},{1,2},{2,3},{3,4},{4,5},{5,6},{6,7},{7,0},{8,9},{9,10},{10,1... | collective-permute-start | bytes 7077896 | tf_op jit(solution)/shard_map/ppermute | solution.py:11
  336.8 51.1 %collective-permute-start.6 = (bf16[768,1536]{1,0:T(8,128)(2,1)}, bf16[768,1536]{1,0:T(8,128)(2,1)}, u32[]{:S(2)}, u32[]{:S(2)}) collective-permute-start(bf16[768,1536]{1,0:T(8,128)(2,1)} %collective-permute-done.5), channel_id=1, source_target_pairs={{0,1},{1,2},{2,3},{3,4},{4,5},{5,6},{6,7},{7,0},{8,9},{9,10},{10,1... | collective-permute-start | bytes 7077896 | tf_op jit(solution)/shard_map/ppermute | solution.py:11
  336.8 67.6 %copy-start.4 = (bf16[768,1536]{1,0:T(8,128)(2,1)S(1)}, bf16[768,1536]{1,0:T(8,128)(2,1)}, u32[]{:S(2)}) copy-start(bf16[768,1536]{1,0:T(8,128)(2,1)} %copy-done.3) | copy-start | bytes 7077892
  336.8 69.2 %copy-start.2 = (bf16[768,1536]{1,0:T(8,128)(2,1)S(1)}, bf16[768,1536]{1,0:T(8,128)(2,1)}, u32[]{:S(2)}) copy-start(bf16[768,1536]{1,0:T(8,128)(2,1)} %copy-done.1) | copy-start | bytes 7077892
  394.5 21.1 %copy-start.6 = (bf16[768,1536]{1,0:T(8,128)(2,1)S(1)}, bf16[768,1536]{1,0:T(8,128)(2,1)}, u32[]{:S(2)}) copy-start(bf16[768,1536]{1,0:T(8,128)(2,1)} %copy-done.5) | copy-start | bytes 7077892
  428.4 380.3 %copy-start.8 = (f32[1536]{0:T(1024)S(1)}, f32[1536]{0:T(1024)}, u32[]{:S(2)}) copy-start(f32[1536]{0:T(1024)} %param.8) | copy-start | bytes 18436
  428.4 380.3 %copy-start.9 = (f32[768]{0:T(1024)S(1)}, f32[768]{0:T(1024)}, u32[]{:S(2)}) copy-start(f32[768]{0:T(1024)} %param.9) | copy-start | bytes 9220
  450.0 538.6 %reduce-scatter.3.cloned.1.call-start = ((), (), s32[]{:S(2)}) async-start(), calls=%async_computation.5 | async-start | bytes 23592960 | tf_op jit(solution)/shard_map/reduce_scatter | solution.py:28
  850.6 206.4 %copy-start.7 = (bf16[1536,768]{1,0:T(8,128)(2,1)S(1)}, bf16[1536,768]{1,0:T(8,128)(2,1)}, u32[]{:S(2)}) copy-start(bf16[1536,768]{1,0:T(8,128)(2,1)} %param.7) | copy-start | bytes 7077892
  850.6 206.3 %all-gather.11.cloned.1.call-start = ((), (), s32[]{:S(2)}) async-start(), calls=%async_computation.6 | async-start | bytes 11796480 | tf_op jit(solution)/shard_map/all_gather | solution.py:34
  992.5 687.9 %reduce-scatter.5.cloned.1.call-start = ((), (), s32[]{:S(2)}) async-start(), calls=%async_computation.7 | async-start | bytes 42467328 | tf_op jit(solution)/shard_map/reduce_scatter | solution.py:36
Sparse Core Ops, SparseCore 0:
  8.9 66.9 all-gather.4
  177.3 65.2 all-gather.8
  450.1 358.5 all-gather.6
  850.7 137.7 reduce-scatter.2
  992.7 64.2 all-gather.10
  1079.6 600.7 reduce-scatter.4
